TPU v7x, 256 devices: a whole 4x4x8 slice. The times are simulated.
256 devices in a mesh: grp: 8 (over y, core), dev: 32 (over x, z).
Axes of the slice: x: 4, y: 4, z: 8, core: 2. Of those that a mesh axis runs over, the one named last changes fastest.
Arguments:
- densities: bfloat16 [256, 200, 200], P(('grp', 'dev')), may hold values from -0.4375 to 0.4375
- core_hamiltonian: bfloat16 [256, 200, 200], P(('grp', 'dev')), may hold values from -0.21875 to 0.21875
- embedding: bfloat16 [256, 200, 200], P(('grp', 'dev')), may hold values from -0.21875 to 0.21875
- fit_factors: bfloat16 [768, 200, 200], P('dev'), may hold values from -0.059814453 to 0.059814453
- orthogonalizers: bfloat16 [256, 200, 200], P(('grp', 'dev'))
- pairs: int32 [3072, 2], replicated, may hold values from 0 to 255, as said below
- assignment: int32 [3072], replicated, may hold values from 0 to 31, as said below
- owner_map: int32 [256], replicated, may hold values from 0 to 255, as said below
Outputs:
- slot_energies: float32 [6144], P(('grp', 'dev'))
- total: float32 [], replicated
Inputs may be any that keep to these rules, and one draw needn't show every extreme that they name: `pairs`: dimer k belongs to group g = k // 384; its first fragment lies in block g, the fragments g * 32 to (g + 1) * 32 - 1, and its second fragment, different from the first, lies in block g or block g + 1 (only block g for the last group). `assignment`: no device receives more than 24 dimers of its group, and in every group some device receives exactly 24. `owner_map`: A permutation of the fragments that maps each block of 32 fragments onto the rows of the same block.
All inputs are finite; a program needn't handle non-finite values.
Results may differ from a plain program's by a relative error of at most 0.0003.
Values may be sent and summed in bfloat16 or wider, within the bound.
No kernel may reach another device: no remote copies, remote signals or barrier semaphores. Data moves between devices by JAX's collectives and lax.ppermute only.
A program may use at most 128 MiB of HBM per device.

v0:
```python
import jax
import jax.numpy as jnp
from jax import lax
from jax.sharding import Mesh
from jax.sharding import PartitionSpec as P

DIM_DEV = 12
SLOTS = 24
DEV = ("dev_0", "dev_1")
GRP_DEV = ("grp", "dev_0", "dev_1")
HALF_WIDTH = 4.0


def laid_out(tiles, dim):
    tiles = jnp.moveaxis(tiles, 0, dim)
    shape = tiles.shape
    return tiles.reshape(*shape[:dim], shape[dim] * shape[dim + 1], *shape[dim + 2 :])


def stacked_from(array, axes, order):
    tiles = array[None]
    for k in order:
        tiles = lax.all_gather(tiles, axes[k], axis=0, tiled=True)
    carried = [lax.axis_size(axes[k]) for k in reversed(order)]
    tiles = tiles.reshape(*carried, *array.shape)
    turned = sorted(range(len(order)), key=lambda place: order[len(order) - 1 - place])
    return tiles.transpose(*turned, *range(len(order), tiles.ndim)).reshape(-1, *array.shape)


def gathered_by_axis(array, axes, order, dim):
    return laid_out(stacked_from(array, axes, order), dim)


def summed_rows(terms, axes):
    total = terms.astype(jnp.bfloat16)
    for axis in axes:
        total = lax.psum_scatter(total, axis, scatter_dimension=0, tiled=True)
    return total.astype(jnp.float32)


def from_behind(block, axis, distance):
    devices = range(lax.axis_size(axis))
    route = [(i - distance, i) for i in devices if i - distance in devices]
    return lax.ppermute(block, axis, route)


def sent_together(arrays, axis, dim, along):
    widths = [a.shape[along] for a in arrays]
    both = jnp.concatenate(arrays, axis=along)
    whole = lax.all_gather(both, axis, axis=dim, tiled=True)
    return tuple(jnp.split(whole, [sum(widths[:k]) for k in range(1, len(widths))], axis=along))


def sent_to_all(array, axis):
    copies = jnp.broadcast_to(array, (lax.axis_size(axis), *array.shape))
    return lax.all_to_all(copies, axis, split_axis=0, concat_axis=0, tiled=True)


def of_everyone(array, axis):
    return sent_to_all(array, axis).sum(axis=0)


def product(left, right):
    return jnp.dot(left, right, preferred_element_type=jnp.float32)


def dimer_energy(fock_i, fock_j, dens_i, dens_j, ortho_i, ortho_j):
    coupling = (0.5 * (product(fock_i, dens_j) + product(dens_i, fock_j))).astype(jnp.bfloat16)
    upper_left = product(fock_i, ortho_i).astype(jnp.bfloat16)
    upper_right = product(coupling, ortho_j).astype(jnp.bfloat16)
    lower_left = product(coupling.T, ortho_i).astype(jnp.bfloat16)
    lower_right = product(fock_j, ortho_j).astype(jnp.bfloat16)
    top_rows = jnp.concatenate(
        [product(ortho_i.T, upper_left), product(ortho_i.T, upper_right)], axis=1
    )
    bottom_rows = jnp.concatenate(
        [product(ortho_j.T, lower_left), product(ortho_j.T, lower_right)], axis=1
    )
    ortho_fock = jnp.concatenate([top_rows, bottom_rows], axis=0)
    size_two = ortho_fock.shape[0]
    half_basis = fock_i.shape[0]
    start = (0.5 * jnp.eye(size_two, dtype=jnp.float32) - ortho_fock / (2.0 * HALF_WIDTH)).astype(
        jnp.bfloat16
    )
    square = product(start, start).astype(jnp.bfloat16)
    cube = product(square, start)
    purified = (3.0 * square.astype(jnp.float32) - 2.0 * cube).astype(jnp.bfloat16)
    left_part = jnp.concatenate(
        [product(ortho_i, purified[:half_basis]), product(ortho_j, purified[half_basis:])], axis=0
    ).astype(jnp.bfloat16)
    new_density = jnp.concatenate(
        [
            product(left_part[:, :half_basis], ortho_i.T),
            product(left_part[:, half_basis:], ortho_j.T),
        ],
        axis=1,
    )
    fock_top = jnp.concatenate([fock_i, coupling], axis=1)
    fock_bottom = jnp.concatenate([coupling.T, fock_j], axis=1)
    dimer_fock = jnp.concatenate([fock_top, fock_bottom], axis=0).astype(jnp.float32)
    monomer_i = jnp.sum(dens_i.astype(jnp.float32) * fock_i.astype(jnp.float32))
    monomer_j = jnp.sum(dens_j.astype(jnp.float32) * fock_j.astype(jnp.float32))
    return jnp.sum(new_density * dimer_fock) - monomer_i - monomer_j


def on_device(
    densities,
    core_hamiltonian,
    embedding,
    fit_factors,
    orthogonalizers,
    pairs,
    assignment,
    owner_map,
):
    members = lax.axis_size(DEV)
    group_index = lax.axis_index("grp")
    member_index = lax.axis_index(DEV)
    basis_size = densities.shape[1]
    aux_count = fit_factors.shape[0]
    flat_fit = fit_factors.reshape(aux_count, basis_size * basis_size)
    gathered = gathered_by_axis(densities, DEV, (0, 1), 0)
    flat_dens = gathered.reshape(members, basis_size * basis_size)
    coeffs = lax.dot_general(
        flat_dens, flat_fit, (((1,), (1,)), ((), ())), preferred_element_type=jnp.float32
    ).astype(jnp.bfloat16)
    coulomb = summed_rows(
        jnp.dot(coeffs, flat_fit, preferred_element_type=jnp.float32).reshape(
            densities.shape[0] * lax.axis_size(DEV), basis_size, basis_size
        ),
        DEV,
    )
    fock_rows = (
        core_hamiltonian.astype(jnp.float32) + embedding.astype(jnp.float32) + coulomb
    ).astype(jnp.bfloat16)
    local_pair = jnp.stack([fock_rows, orthogonalizers], axis=1)
    monomer = jnp.stack([fock_rows, densities, orthogonalizers], axis=1)
    following = from_behind(monomer, "grp", -1)
    own_pair, next_pool = sent_together((local_pair, following), DEV, 0, 1)
    dim_group = DIM_DEV * members
    group_pairs = lax.dynamic_slice_in_dim(pairs, group_index * dim_group, dim_group, 0)
    group_assign = lax.dynamic_slice_in_dim(assignment, group_index * dim_group, dim_group, 0)
    is_mine = group_assign == member_index
    mine_count = is_mine.astype(jnp.int32)
    before = jnp.cumsum(mine_count) - mine_count
    select = is_mine[None, :] & (before[None, :] == jnp.arange(SLOTS, dtype=jnp.int32)[:, None])
    list_positions = jnp.arange(dim_group, dtype=jnp.int32)

    def energy_of(listed):
        pair_ids = group_pairs[listed]
        first_row = owner_map[pair_ids[0]] - group_index * members
        second_row = owner_map[pair_ids[1]] - group_index * members
        in_next = second_row >= members
        pool_row = jnp.where(in_next, second_row - members, second_row)
        first_pair = own_pair[first_row]
        own_second = own_pair[pool_row]
        next_second = next_pool[pool_row]
        second_fock = jnp.where(in_next, next_second[0], own_second[0])
        second_dens = jnp.where(in_next, next_second[1], gathered[pool_row])
        second_ortho = jnp.where(in_next, next_second[2], own_second[1])
        return dimer_energy(
            first_pair[0],
            second_fock,
            gathered[first_row],
            second_dens,
            first_pair[1],
            second_ortho,
        )

    listed = member_index * DIM_DEV + jnp.arange(DIM_DEV, dtype=jnp.int32)
    values = lax.map(energy_of, listed)
    spread = jnp.sum(
        jnp.where(list_positions[None, :] == listed[:, None], values[:, None], 0.0), axis=0
    )
    group_values = of_everyone(spread, DEV)
    slot_energies = jnp.sum(jnp.where(select, group_values[None, :], 0.0), axis=1)
    energy_sum = of_everyone(jnp.sum(group_values), "grp")
    return (slot_energies, energy_sum)


def solution(mesh):
    torus = Mesh(mesh.devices.reshape(mesh.shape["grp"], 4, 8), ("grp", "dev_0", "dev_1"))
    in_specs = (
        P(GRP_DEV, None, None),
        P(GRP_DEV, None, None),
        P(GRP_DEV, None, None),
        P(DEV, None, None),
        P(GRP_DEV, None, None),
        P(),
        P(),
        P(),
    )
    out_specs = (P(GRP_DEV), P())
    return jax.shard_map(
        on_device, mesh=torus, in_specs=in_specs, out_specs=out_specs, check_vma=False
    )
```

profile of v0, /device:TPU:1, one launch (start us, length us, event | category | flops | bytes accessed | tf_op | source)
XLA Modules:
  0.0 740.4 jit_solution(16473954267569400295)
XLA Ops:
  7.2 12.8 %all-gather = bf16[4,200,200]{2,1,0:T(8,128)(2,1)} all-gather(bf16[1,200,200]{2,1,0:T(8,128)(2,1)} %param.10), channel_id=2, replica_groups=mesh['grp'=8,'dev_0'=4,'dev_1'=8] {'dev_0'}, dimensions={0}, use_global_device_ids=true | all-gather | bytes 400000 | tf_op jit(solution)/shard_map/all_gather | solution.py:23
  20.1 3.9 reshape.83
  24.1 5.0 dot_general.108
  29.1 41.3 %all-gather.7.cloned.1.call-done = bf16[32,200,200]{2,1,0:T(8,128)(2,1)} async-done(((bf16[4,200,200]{2,1,0:T(8,128)(2,1)}), bf16[32,200,200]{2,1,0:T(8,128)(2,1)}) %all-gather.7.cloned.1.call-update) | async-done | bytes 2560016 | tf_op jit(solution)/shard_map/all_gather | solution.py:23
  70.4 2.1 copy.62
  72.6 4.1 reshape_reshape_reshape.3
  76.6 8.2 %fusion.41 = bf16[32,200,200]{2,0,1:T(8,128)(2,1)} fusion(bf16[200,200,24]{1,0,2:T(8,128)(2,1)} %dot_general.108, bf16[32,40000]{1,0:T(8,128)(2,1)} %reshape_reshape_reshape.3, bf16[24,40000]{1,0:T(8,128)(2,1)} %copy-done.2), kind=kOutput, calls=%fused_computation.64 | convolution fusion | flops 124160768 | bytes 8960000 | tf_op jit(solution)/shard_map/dot_general | solution.py:128
  86.7 79.8 %all-reduce.3.cloned.1.call-done = bf16[32,200,200]{2,0,1:T(8,128)(2,1)} async-done(((bf16[32,200,200]{2,0,1:T(8,128)(2,1)}), bf16[32,200,200]{2,0,1:T(8,128)(2,1)}) %all-reduce.3.cloned.1.call-update) | async-done | bytes 2560016
  168.8 33.8 %reduce-scatter.3.cloned.1.call-done = bf16[1,200,200]{2,1,0:T(8,128)(2,1)} async-done(((bf16[8,200,200]{2,1,0:T(8,128)(2,1)}), bf16[1,200,200]{2,1,0:T(8,128)(2,1)}) %reduce-scatter.3.cloned.1.call-update) | async-done | bytes 80016 | tf_op jit(solution)/shard_map/reduce_scatter | solution.py:37
  203.8 7.6 %collective-permute-start = (bf16[1,3,200,200]{3,2,1,0:T(8,128)(2,1)S(1)}, bf16[1,3,200,200]{3,2,1,0:T(8,128)(2,1)S(1)}, u32[]{:S(2)}, u32[]{:S(2)}) collective-permute-start(bf16[1,3,200,200]{3,2,1,0:T(8,128)(2,1)S(1)} %pad_maximum_fusion.3), channel_id=1, source_target_pairs={{32,0},{64,32},{96,64},{128,96},{160,128},{192,160},{224,192},{33,... | collective-permute-start | bytes 720008 | tf_op jit(solution)/shard_map/ppermute | solution.py:44
  211.4 5.4 collective-permute-done
  219.1 4.0 copy.42
  223.1 130.0 %all-gather.5.cloned.1.call-done = bf16[32,5,200,200]{3,2,1,0:T(8,128)(2,1)} async-done(((bf16[1,5,200,200]{3,2,1,0:T(8,128)(2,1)}), bf16[32,5,200,200]{3,2,1,0:T(8,128)(2,1)}) %all-gather.5.cloned.1.call-update) | async-done | bytes 12800016 | tf_op jit(solution)/shard_map/all_gather | solution.py:50
  353.1 6.0 split.8
  359.1 10.3 %copy.43 = bf16[32,2,200,200]{2,3,1,0:T(8,128)(2,1)} copy(bf16[32,2,200,200]{3,2,1,0:T(8,128)(2,1)} %split.8) | data formatting | bytes 10240000 | tf_op jit(solution)/shard_map/while | solution.py:171
  369.3 8.2 %split.9 = bf16[32,3,200,200]{3,2,1,0:T(8,128)(2,1)} slice(bf16[32,5,200,200]{3,2,1,0:T(8,128)(2,1)} %all-gather.5.cloned.1.call-done), slice={[0:32], [2:5], [0:200], [0:200]} | slice | bytes 15360000 | tf_op jit(solution)/shard_map/split | solution.py:51
  377.5 327.1 %while.12 = (s32[]{:T(128)}, f32[12]{0:T(128)S(1)}, s32[12]{0:T(128)S(1)}, s32[384,2]{0,1:T(2,128)S(1)}, s32[256]{0:T(256)S(1)}, /*index=5*/s32[]{:T(128)}, bf16...) while((s32[]{:T(128)}, f32[12]{0:T(128)S(1)}, ...), condition=%wide.region_8.9_spmd, body=%wide.region_4.8_spmd.sunk | while | flops 550840000 | bytes 10055895 | solution.py:171
  388.9 1.8 multiply_reduce_fusion.3
  470.7 1.8 multiply_reduce_fusion.3
  552.5 1.8 multiply_reduce_fusion.3
  705.4 5.4 all-to-all-start
  710.8 8.7 %all-to-all-done = f32[32,1,384]{2,1,0:T(1,128)S(1)} async-done(((f32[32,1,384]{2,1,0:T(1,128)}), f32[32,1,384]{2,1,0:T(1,128)S(1)}, u32[]{:S(2)}, u32[]{:S(2)}) %all-to-all-start) | async-done | bytes 49184 | tf_op jit(solution)/shard_map/all_to_all | solution.py:56
  721.5 7.2 all-to-all-start.1
  729.3 4.0 all-to-all-done.1
  (340 shorter events, 223.2 us)
Async XLA Ops:
  7.2 211.8 %copy-start = (s32[3072,2]{0,1:T(2,128)S(1)}, s32[3072,2]{0,1:T(2,128)}, u32[]{:S(2)}) copy-start(s32[3072,2]{0,1:T(2,128)} %param.15) | copy-start | bytes 73732
  7.2 63.2 %all-gather.7.cloned.1.call-start = ((), (), s32[]{:S(2)}) async-start(), calls=%async_computation.5 | async-start | bytes 3686400 | tf_op jit(solution)/shard_map/all_gather | solution.py:23
  20.1 146.4 %all-reduce.3.cloned.1.call-start = ((), (), s32[]{:S(2)}) async-start(), calls=%async_computation.6 | async-start | bytes 6553600
  24.0 46.4 %copy-start.2 = (bf16[24,40000]{1,0:T(8,128)(2,1)}, bf16[24,40000]{1,0:T(8,128)(2,1)S(1)}, u32[]{:S(2)}) copy-start(bf16[24,40000]{1,0:T(8,128)(2,1)S(1)} %reshape.83) | copy-start | bytes 5760004
  84.8 0.7 copy-start.6
  84.8 118.9 %copy-start.3 = (bf16[1,200,200]{2,1,0:T(8,128)(2,1)S(1)}, bf16[1,200,200]{2,1,0:T(8,128)(2,1)}, u32[]{:S(2)}) copy-start(bf16[1,200,200]{2,1,0:T(8,128)(2,1)} %param.10) | copy-start | bytes 240004
  84.8 118.9 %copy-start.4 = (bf16[1,200,200]{2,1,0:T(8,128)(2,1)S(1)}, bf16[1,200,200]{2,1,0:T(8,128)(2,1)}, u32[]{:S(2)}) copy-start(bf16[1,200,200]{2,1,0:T(8,128)(2,1)} %param.14) | copy-start | bytes 240004
  84.8 117.8 %reduce-scatter.3.cloned.1.call-start = ((), (), s32[]{:S(2)}) async-start(), calls=%async_computation.3 | async-start | bytes 921600 | tf_op jit(solution)/shard_map/reduce_scatter | solution.py:37
  168.8 184.3 %all-gather.5.cloned.1.call-start = ((), (), s32[]{:S(2)}) async-start(), calls=%async_computation.4 | async-start | bytes 16896000 | tf_op jit(solution)/shard_map/all_gather | solution.py:50
  203.8 13.0 %collective-permute-start = (bf16[1,3,200,200]{3,2,1,0:T(8,128)(2,1)S(1)}, bf16[1,3,200,200]{3,2,1,0:T(8,128)(2,1)S(1)}, u32[]{:S(2)}, u32[]{:S(2)}) collective-permute-start(bf16[1,3,200,200]{3,2,1,0:T(8,128)(2,1)S(1)} %pad_maximum_fusion.3), channel_id=1, source_target_pairs={{32,0},{64,32},{96,64},{128,96},{160,128},{192,160},{224,192},{33,... | collective-permute-start | bytes 720008 | tf_op jit(solution)/shard_map/ppermute | solution.py:44
  369.3 8.2 %copy-start.5 = (s32[256]{0:T(256)S(1)}, s32[256]{0:T(256)}, u32[]{:S(2)}) copy-start(s32[256]{0:T(256)} %param.17) | copy-start | bytes 3076
  704.6 29.2 %copy-start.1 = (s32[3072,2]{0,1:T(2,128)S(1)}, s32[3072,2]{0,1:T(2,128)}, u32[]{:S(2)}) copy-start(s32[3072,2]{0,1:T(2,128)} %param.15) | copy-start | bytes 73732
  705.4 14.2 %all-to-all-start = ((f32[32,1,384]{2,1,0:T(1,128)}), f32[32,1,384]{2,1,0:T(1,128)S(1)}, u32[]{:S(2)}, u32[]{:S(2)}) async-start(f32[32,1,384]{2,1,0:T(1,128)} %broadcast_in_dim.50), calls=%async_computation.1 | async-start | bytes 98304 | tf_op jit(solution)/shard_map/all_to_all | solution.py:56
  721.5 11.8 %all-to-all-start.1 = ((f32[8,1,1]{2,1,0:T(1,128)}), f32[8,1,1]{2,1,0:T(1,128)S(1)}, u32[]{:S(2)}, u32[]{:S(2)}) async-start(f32[8,1,1]{2,1,0:T(1,128)} %broadcast_in_dim.53), calls=%async_computation.2 | async-start | bytes 8192 | tf_op jit(solution)/shard_map/all_to_all | solution.py:56
Sparse Core Ops, SparseCore 0:
  20.2 50.1 all-gather.6
  84.9 81.5 all-reduce.2
  169.0 33.5 reduce-scatter.2
  217.9 135.1 all-gather.4
where the time goes:
time: 746 us; the launch traced here: 740 us
  waiting for transfers between devices  303 us (41%)
  matrix products  140 us (19%)
  loops' own time  109 us (15%)
  local copies, waits for them, and re-layouts  91.6 us (12%)
  other arithmetic  49 us (7%)
  starting transfers between devices  20.3 us (3%)
  between operations  14.5 us (2%)
  blocking collectives  12.8 us (2%)
    dot_general x144, matrix products, product(): return jnp.dot(left, right, preferred_element_type=jnp.float32)  131 us
    all_gather x1, waiting for transfers between devices, sent_together(): whole = lax.all_gather(both, axis, axis=dim, tiled=True)  130 us
    another operation x1, loops' own time, on_device(): values = lax.map(energy_of, listed)  109 us
    unnamed x5, waiting for transfers between devices  79.9 us
    all_gather x1, waiting for transfers between devices, stacked_from(): tiles = lax.all_gather(tiles, axes[k], axis=0, tiled=True)  41.3 us
    reduce_scatter x1, waiting for transfers between devices, summed_rows(): total = lax.psum_scatter(total, axis, scatter_dimension=0, tiled=True)  33.8 us
    reduce_sum x12, other arithmetic, dimer_energy(): monomer_j = jnp.sum(dens_j.astype(jnp.float32) * fock_j.astype(jnp.float32))  22.1 us
  transfers between devices with their start and end apart: 7, of which 7 were waited for; matrix products, arithmetic and copies ran while one was open for 2% of the time, Pallas kernels for 0%

commit v1 on v0

--- a/solution.py
+++ b/solution.py
@@ -20,7 +20,9 @@
 def stacked_from(array, axes, order):
     tiles = array[None]
     for k in order:
-        tiles = lax.all_gather(tiles, axes[k], axis=0, tiled=True)
+        tiles = jnp.concatenate(
+            lax.all_to_all(jnp.stack([tiles] * lax.axis_size(axes[k])), axes[k], 0, 0), axis=0
+        )
     carried = [lax.axis_size(axes[k]) for k in reversed(order)]
     tiles = tiles.reshape(*carried, *array.shape)
     turned = sorted(range(len(order)), key=lambda place: order[len(order) - 1 - place])

time: 746 us -> 779 us (1.044)
  waiting for transfers between devices: 303 us -> 325 us
  starting transfers between devices: 20.3 us -> 28.4 us
    all_to_all x0 -> x1, waiting for transfers between devices: none -> 68.1 us  [stacked_from(): lax.all_to_all(jnp.stack([tiles] * lax.axis_size(axes[k])), axes[k], 0, 0)]
    all_gather x1 -> x0, waiting for transfers between devices: 41.3 us -> none  [stacked_from(): tiles = lax.all_gather(tiles, axes[k], axis=0, tiled=True)]
    all_gather x1 -> x0, blocking collectives: 12.8 us -> none  [stacked_from(): tiles = lax.all_gather(tiles, axes[k], axis=0, tiled=True)]
    all_to_all x0 -> x1, blocking collectives: none -> 11.9 us  [stacked_from(): lax.all_to_all(jnp.stack([tiles] * lax.axis_size(axes[k])), axes[k], 0, 0)]
    all_to_all x0 -> x1, starting transfers between devices: none -> 8.19 us  [stacked_from(): lax.all_to_all(jnp.stack([tiles] * lax.axis_size(axes[k])), axes[k], 0, 0)]
    unnamed x5 -> x4, waiting for transfers between devices: 79.9 us -> 75.5 us
where the time goes in v1:
time: 779 us; the launch traced here: 773 us
  waiting for transfers between devices  325 us (42%)
  matrix products  140 us (18%)
  loops' own time  109 us (14%)
  local copies, waits for them, and re-layouts  94.9 us (12%)
  other arithmetic  49 us (6%)
  starting transfers between devices  28.4 us (4%)
  between operations  14.5 us (2%)
  blocking collectives  11.9 us (2%)
    dot_general x144, matrix products, product(): return jnp.dot(left, right, preferred_element_type=jnp.float32)  131 us
    all_gather x1, waiting for transfers between devices, sent_together(): whole = lax.all_gather(both, axis, axis=dim, tiled=True)  130 us
    another operation x1, loops' own time, on_device(): values = lax.map(energy_of, listed)  109 us
    unnamed x4, waiting for transfers between devices  75.5 us
    all_to_all x1, waiting for transfers between devices, stacked_from(): lax.all_to_all(jnp.stack([tiles] * lax.axis_size(axes[k])), axes[k], 0, 0)  68.1 us
    reduce_scatter x1, waiting for transfers between devices, summed_rows(): total = lax.psum_scatter(total, axis, scatter_dimension=0, tiled=True)  33.8 us
    reduce_sum x12, other arithmetic, dimer_energy(): monomer_j = jnp.sum(dens_j.astype(jnp.float32) * fock_j.astype(jnp.float32))  22.1 us
  transfers between devices with their start and end apart: 7, of which 7 were waited for; matrix products, arithmetic and copies ran while one was open for 2% of the time, Pallas kernels for 0%

profile of v1, /device:TPU:1, one launch (start us, length us, event | category | flops | bytes accessed | tf_op | source)
XLA Modules:
  0.0 772.8 jit_solution(11169452635058588679)
XLA Ops:
  8.1 11.9 %all_to_all.22 = bf16[4,1,1,200,200]{4,3,2,1,0:T(8,128)(2,1)S(1)} all-to-all(bf16[4,1,1,200,200]{4,3,2,1,0:T(8,128)(2,1)S(1)} %stack.20), channel_id=1, replica_groups=mesh['grp'=8,'dev_0'=4,'dev_1'=8] {'dev_0'}, dimensions={0} | all-to-all | bytes 640000 | tf_op jit(solution)/shard_map/all_to_all | solution.py:24
  20.0 1.9 stack.21
  21.9 8.2 %all-to-all-start.1 = ((bf16[8,4,1,200,200]{4,3,1,2,0:T(8,128)(2,1)}), bf16[8,4,1,200,200]{4,3,1,2,0:T(8,128)(2,1)}, u32[]{:S(2)}, u32[]{:S(2)}) async-start(bf16[8,4,1,200,200]{4,3,1,2,0:T(8,128)(2,1)} %stack.21), calls=%async_computation.1 | async-start | bytes 6553600 | tf_op jit(solution)/shard_map/all_to_all | solution.py:24
  30.1 3.9 reshape.86
  34.1 5.1 dot_general.108
  39.2 68.1 %all-to-all-done.1 = bf16[8,4,1,200,200]{4,3,1,2,0:T(8,128)(2,1)} async-done(((bf16[8,4,1,200,200]{4,3,1,2,0:T(8,128)(2,1)}), bf16[8,4,1,200,200]{4,3,1,2,0:T(8,128)(2,1)}, u32[]{:S(2)}, u32[]{:S(2)}) %all-to-all-start.1) | async-done | bytes 2560032 | tf_op jit(solution)/shard_map/all_to_all | solution.py:24
  107.2 2.1 copy.68
  109.4 4.1 reshape_reshape_reshape.3
  113.4 8.2 %fusion.41 = bf16[32,200,200]{2,0,1:T(8,128)(2,1)} fusion(bf16[200,200,24]{1,0,2:T(8,128)(2,1)} %dot_general.108, bf16[32,40000]{1,0:T(8,128)(2,1)} %reshape_reshape_reshape.3, bf16[24,40000]{1,0:T(8,128)(2,1)} %copy-done.2), kind=kOutput, calls=%fused_computation.63 | convolution fusion | flops 124160768 | bytes 8960000 | tf_op jit(solution)/shard_map/dot_general | solution.py:130
  123.5 75.5 %all-reduce.3.cloned.1.call-done = bf16[32,200,200]{2,0,1:T(8,128)(2,1)} async-done(((bf16[32,200,200]{2,0,1:T(8,128)(2,1)}), bf16[32,200,200]{2,0,1:T(8,128)(2,1)}) %all-reduce.3.cloned.1.call-update) | async-done | bytes 2560016
  201.3 33.8 %reduce-scatter.3.cloned.1.call-done = bf16[1,200,200]{2,1,0:T(8,128)(2,1)} async-done(((bf16[8,200,200]{2,1,0:T(8,128)(2,1)}), bf16[1,200,200]{2,1,0:T(8,128)(2,1)}) %reduce-scatter.3.cloned.1.call-update) | async-done | bytes 80016 | tf_op jit(solution)/shard_map/reduce_scatter | solution.py:39
  236.2 7.6 collective-permute-start
  243.8 5.4 collective-permute-done
  251.5 4.4 copy.49
  255.9 129.6 %all-gather.2.cloned.1.call-done = bf16[32,5,200,200]{3,2,1,0:T(8,128)(2,1)} async-done(((bf16[1,5,200,200]{3,2,1,0:T(8,128)(2,1)}), bf16[32,5,200,200]{3,2,1,0:T(8,128)(2,1)}) %all-gather.2.cloned.1.call-update) | async-done | bytes 12800016 | tf_op jit(solution)/shard_map/all_gather | solution.py:52
  385.5 6.0 split.8
  391.5 10.3 %copy.47 = bf16[32,2,200,200]{2,3,1,0:T(8,128)(2,1)} copy(bf16[32,2,200,200]{3,2,1,0:T(8,128)(2,1)} %split.8) | data formatting | bytes 10240000 | tf_op jit(solution)/shard_map/while | solution.py:173
  401.8 8.2 %split.9 = bf16[32,3,200,200]{3,2,1,0:T(8,128)(2,1)} slice(bf16[32,5,200,200]{3,2,1,0:T(8,128)(2,1)} %all-gather.2.cloned.1.call-done), slice={[0:32], [2:5], [0:200], [0:200]} | slice | bytes 15360000 | tf_op jit(solution)/shard_map/split | solution.py:53
  410.0 327.1 %while.12 = (s32[]{:T(128)}, f32[12]{0:T(128)S(1)}, s32[12]{0:T(128)S(1)}, s32[384,2]{0,1:T(2,128)S(1)}, s32[256]{0:T(256)S(1)}, /*index=5*/s32[]{:T(128)}, bf16...) while((s32[]{:T(128)}, f32[12]{0:T(128)S(1)}, ...), condition=%wide.region_8.9_spmd, body=%wide.region_4.8_spmd.sunk | while | flops 550840000 | bytes 10055895 | solution.py:173
  421.3 1.8 multiply_reduce_fusion.3
  737.8 5.4 all-to-all-start.2
  743.2 8.7 %all-to-all-done.2 = f32[32,1,384]{2,1,0:T(1,128)S(1)} async-done(((f32[32,1,384]{2,1,0:T(1,128)}), f32[32,1,384]{2,1,0:T(1,128)S(1)}, u32[]{:S(2)}, u32[]{:S(2)}) %all-to-all-start.2) | async-done | bytes 49184 | tf_op jit(solution)/shard_map/all_to_all | solution.py:58
  753.9 7.2 all-to-all-start.3
  761.7 4.0 all-to-all-done.3
  (341 shorter events, 227.8 us)
Async XLA Ops:
  7.2 244.2 %copy-start = (s32[3072,2]{0,1:T(2,128)S(1)}, s32[3072,2]{0,1:T(2,128)}, u32[]{:S(2)}) copy-start(s32[3072,2]{0,1:T(2,128)} %param.15) | copy-start | bytes 73732
  21.9 85.3 %all-to-all-start.1 = ((bf16[8,4,1,200,200]{4,3,1,2,0:T(8,128)(2,1)}), bf16[8,4,1,200,200]{4,3,1,2,0:T(8,128)(2,1)}, u32[]{:S(2)}, u32[]{:S(2)}) async-start(bf16[8,4,1,200,200]{4,3,1,2,0:T(8,128)(2,1)} %stack.21), calls=%async_computation.1 | async-start | bytes 6553600 | tf_op jit(solution)/shard_map/all_to_all | solution.py:24
  30.1 168.8 %all-reduce.3.cloned.1.call-start = ((), (), s32[]{:S(2)}) async-start(), calls=%async_computation.7 | async-start | bytes 6553600
  34.1 5.1 copy-start.2
  121.6 0.7 copy-start.6
  121.6 114.5 %copy-start.3 = (bf16[1,200,200]{2,1,0:T(8,128)(2,1)S(1)}, bf16[1,200,200]{2,1,0:T(8,128)(2,1)}, u32[]{:S(2)}) copy-start(bf16[1,200,200]{2,1,0:T(8,128)(2,1)} %param.10) | copy-start | bytes 240004
  121.6 114.5 %copy-start.4 = (bf16[1,200,200]{2,1,0:T(8,128)(2,1)S(1)}, bf16[1,200,200]{2,1,0:T(8,128)(2,1)}, u32[]{:S(2)}) copy-start(bf16[1,200,200]{2,1,0:T(8,128)(2,1)} %param.14) | copy-start | bytes 240004
  121.6 113.5 %reduce-scatter.3.cloned.1.call-start = ((), (), s32[]{:S(2)}) async-start(), calls=%async_computation.5 | async-start | bytes 921600 | tf_op jit(solution)/shard_map/reduce_scatter | solution.py:39
  201.2 184.3 %all-gather.2.cloned.1.call-start = ((), (), s32[]{:S(2)}) async-start(), calls=%async_computation.6 | async-start | bytes 16896000 | tf_op jit(solution)/shard_map/all_gather | solution.py:52
  236.2 13.0 %collective-permute-start = (bf16[1,3,200,200]{3,2,1,0:T(8,128)(2,1)S(1)}, bf16[1,3,200,200]{3,2,1,0:T(8,128)(2,1)S(1)}, u32[]{:S(2)}, u32[]{:S(2)}) collective-permute-start(bf16[1,3,200,200]{3,2,1,0:T(8,128)(2,1)S(1)} %pad_maximum_fusion.3), channel_id=1, source_target_pairs={{32,0},{64,32},{96,64},{128,96},{160,128},{192,160},{224,192},{33,... | collective-permute-start | bytes 720008 | tf_op jit(solution)/shard_map/ppermute | solution.py:46
  401.8 8.2 %copy-start.5 = (s32[256]{0:T(256)S(1)}, s32[256]{0:T(256)}, u32[]{:S(2)}) copy-start(s32[256]{0:T(256)} %param.17) | copy-start | bytes 3076
  737.1 29.2 %copy-start.1 = (s32[3072,2]{0,1:T(2,128)S(1)}, s32[3072,2]{0,1:T(2,128)}, u32[]{:S(2)}) copy-start(s32[3072,2]{0,1:T(2,128)} %param.15) | copy-start | bytes 73732
  737.8 14.2 %all-to-all-start.2 = ((f32[32,1,384]{2,1,0:T(1,128)}), f32[32,1,384]{2,1,0:T(1,128)S(1)}, u32[]{:S(2)}, u32[]{:S(2)}) async-start(f32[32,1,384]{2,1,0:T(1,128)} %broadcast_in_dim.46), calls=%async_computation.3 | async-start | bytes 98304 | tf_op jit(solution)/shard_map/all_to_all | solution.py:58
  753.9 11.8 %all-to-all-start.3 = ((f32[8,1,1]{2,1,0:T(1,128)}), f32[8,1,1]{2,1,0:T(1,128)S(1)}, u32[]{:S(2)}, u32[]{:S(2)}) async-start(f32[8,1,1]{2,1,0:T(1,128)} %broadcast_in_dim.49), calls=%async_computation.4 | async-start | bytes 8192 | tf_op jit(solution)/shard_map/all_to_all | solution.py:58
Sparse Core Ops, SparseCore 0:
  121.7 77.1 all-reduce.2
  201.5 33.5 reduce-scatter.2
  250.3 135.1 all-gather.1
